TPU v7x, 32 devices: a whole 2x2x4 slice. The times are simulated.
32 devices in a mesh: dp: 8 (over y, x, core), mp: 4 (over z).
Axes of the slice: x: 2, y: 2, z: 4, core: 2. Of those that a mesh axis runs over, the one named last changes fastest.
Arguments:
- tokens: bfloat16 [8192, 2048], P('dp'), may hold values from -6 to 6
- doc_ids: int32 [16, 512], P('dp'), may hold values from 0 to 3, never falling along the last dimension, each value on 1 to 256 neighbouring positions
- selection: int32 [16, 512], P('dp'), may hold values 0 or 1
- w_query: bfloat16 [2048, 2048], P('dp', 'mp'), may hold values from -0.125 to 0.125
- w_key: bfloat16 [2048, 256], P('dp', 'mp'), may hold values from -0.125 to 0.125
- w_value: bfloat16 [2048, 256], P('dp', 'mp'), may hold values from -0.125 to 0.125
- w_out: bfloat16 [2048, 2048], P('mp', 'dp'), may hold values from -0.375 to 0.375
- w_gate: bfloat16 [2048, 5632], P('dp', 'mp'), may hold values from -0.125 to 0.125
- w_up: bfloat16 [2048, 5632], P('dp', 'mp'), may hold values from -0.125 to 0.125
- w_down: bfloat16 [5632, 2048], P('mp', 'dp'), may hold values from -0.078125 to 0.078125
- attn_gain: bfloat16 [2048], P('dp'), may hold values from 0.25 to 1.75
- mlp_gain: bfloat16 [2048], P('dp'), may hold values from 0.25 to 1.75
- cotangent: bfloat16 [8192, 2048], P('dp'), may hold values from -6 to 6
Outputs:
- output: bfloat16 [8192, 2048], P('dp')
- input_grad: float32 [8192, 2048], P('dp')
- grad_w_query: float32 [2048, 2048], P('dp', 'mp')
- grad_w_key: float32 [2048, 256], P('dp', 'mp')
- grad_w_value: float32 [2048, 256], P('dp', 'mp')
- grad_w_out: float32 [2048, 2048], P('mp', 'dp')
- grad_w_gate: float32 [2048, 5632], P('dp', 'mp')
- grad_w_up: float32 [2048, 5632], P('dp', 'mp')
- grad_w_down: float32 [5632, 2048], P('mp', 'dp')
- grad_attn_gain: float32 [2048], P('dp')
- grad_mlp_gain: float32 [2048], P('dp')
Inputs may be any that keep to these rules, and one draw needn't show every extreme that they name: `doc_ids`: within a sequence the ids never fall; a document spans 1 to 256 tokens and one spans exactly 256.
All inputs are finite; a program needn't handle non-finite values. No bound on the sum of `selection` on one device may be relied on, other than what follows from the above.
Results may differ from a plain program's by a relative error of at most 0.024.
Values may be sent and summed in bfloat16 or wider, within the bound.
A program may use at most 256 MiB of HBM per device.

v0:
```python
import jax
import jax.numpy as jnp
from jax import lax
from jax.sharding import PartitionSpec as P

HEAD_DIM = 64
EPSILON = 1e-05
MASKED = -1e30


def rope_tables(length, head_width):
    half_width = head_width // 2
    frequency = 10000.0 ** (-2.0 * jnp.arange(half_width, dtype=jnp.float32) / head_width)
    places = jnp.arange(length, dtype=jnp.float32)
    angles = places[:, None] * frequency[None, :]
    return (jnp.cos(angles)[:, None, :], jnp.sin(angles)[:, None, :])


def rotate(field, cosine_table, sine_table):
    half_width = field.shape[-1] // 2
    first_half = field[..., :half_width]
    second_half = field[..., half_width:]
    return jnp.concatenate(
        [
            first_half * cosine_table - second_half * sine_table,
            second_half * cosine_table + first_half * sine_table,
        ],
        axis=-1,
    )


def allowed_pairs(doc_row):
    length = doc_row.shape[0]
    query_index = lax.broadcasted_iota(jnp.int32, (length, length), 0)
    key_index = lax.broadcasted_iota(jnp.int32, (length, length), 1)
    return (doc_row[:, None] == doc_row[None, :]) & (query_index >= key_index)


def rms_forward(residual, gain_row):
    inverse = lax.rsqrt(jnp.mean(residual * residual, axis=-1, keepdims=True) + EPSILON)
    return (residual * inverse * gain_row, inverse)


def rms_backward(residual, inverse, gain_row, grad_normed):
    scaled = grad_normed * gain_row
    gain_part = jnp.sum(grad_normed * residual * inverse, axis=0)
    mean_term = jnp.mean(scaled * residual, axis=-1, keepdims=True)
    return (inverse * scaled - residual * (inverse * inverse * inverse) * mean_term, gain_part)


def attend_forward(queries, key_rows, value_rows, doc_row, score_scale):
    length, kv_local, head_width = key_rows.shape
    grouped = queries.reshape(length, kv_local, -1, head_width)
    scores = (
        jnp.einsum("qkgd,skd->kgqs", grouped, key_rows, preferred_element_type=jnp.float32)
        * score_scale
    )
    scores = jnp.where(allowed_pairs(doc_row), scores, MASKED)
    highest = jnp.max(scores, axis=-1, keepdims=True)
    shifted_exp = jnp.exp(scores - highest)
    totals = jnp.sum(shifted_exp, axis=-1, keepdims=True)
    probs_low = (shifted_exp / totals).astype(jnp.bfloat16)
    mixed_heads = jnp.einsum(
        "kgqs,skd->qkgd", probs_low, value_rows, preferred_element_type=jnp.float32
    )
    return (mixed_heads.reshape(length, -1), highest + jnp.log(totals))


def attend_backward(queries, key_rows, value_rows, doc_row, logsum, grad_mixed, score_scale):
    length, kv_local, head_width = key_rows.shape
    grouped = queries.reshape(length, kv_local, -1, head_width)
    grad_grouped = grad_mixed.reshape(length, kv_local, -1, head_width)
    scores = (
        jnp.einsum("qkgd,skd->kgqs", grouped, key_rows, preferred_element_type=jnp.float32)
        * score_scale
    )
    attn_probs = jnp.where(allowed_pairs(doc_row), jnp.exp(scores - logsum), 0.0)
    grad_probs = jnp.einsum(
        "qkgd,skd->kgqs", grad_grouped, value_rows, preferred_element_type=jnp.float32
    )
    inner_sum = jnp.sum(attn_probs * grad_probs, axis=-1, keepdims=True)
    grad_scores = (attn_probs * (grad_probs - inner_sum)).astype(jnp.bfloat16)
    grad_queries = (
        jnp.einsum("kgqs,skd->qkgd", grad_scores, key_rows, preferred_element_type=jnp.float32)
        * score_scale
    )
    grad_keys = (
        jnp.einsum("kgqs,qkgd->skd", grad_scores, grouped, preferred_element_type=jnp.float32)
        * score_scale
    )
    grad_values = jnp.einsum(
        "kgqs,qkgd->skd",
        attn_probs.astype(jnp.bfloat16),
        grad_grouped,
        preferred_element_type=jnp.float32,
    )
    return (grad_queries.reshape(length, -1, head_width), grad_keys, grad_values)


def per_device(
    tokens,
    doc_ids,
    selection,
    w_query,
    w_key,
    w_value,
    w_out,
    w_gate,
    w_up,
    w_down,
    attn_gain,
    mlp_gain,
    cotangent,
):
    (
        full_query,
        full_key,
        full_value,
        full_out,
        full_gate,
        full_up,
        full_down,
        gathered_one,
        gathered_two,
    ) = (
        lax.all_gather(w_query, "dp", axis=0, tiled=True),
        lax.all_gather(w_key, "dp", axis=0, tiled=True),
        lax.all_gather(w_value, "dp", axis=0, tiled=True),
        lax.all_gather(w_out, "dp", axis=1, tiled=True),
        lax.all_gather(w_gate, "dp", axis=0, tiled=True),
        lax.all_gather(w_up, "dp", axis=0, tiled=True),
        lax.all_gather(w_down, "dp", axis=1, tiled=True),
        lax.all_gather(attn_gain, "dp", axis=0, tiled=True),
        lax.all_gather(mlp_gain, "dp", axis=0, tiled=True),
    )
    gain_one = gathered_one.astype(jnp.float32)
    gain_two = gathered_two.astype(jnp.float32)
    seq_local, length = doc_ids.shape
    tok_local = seq_local * length
    heads_local = full_query.shape[1] // HEAD_DIM
    kv_local = full_key.shape[1] // HEAD_DIM
    score_scale = HEAD_DIM ** (-0.5)
    cosine_table, sine_table = rope_tables(length, HEAD_DIM)
    residual = tokens.astype(jnp.float32)
    normed_float, inverse_one = rms_forward(residual, gain_one)
    normed_one = normed_float.astype(jnp.bfloat16)
    query_lin = jnp.dot(normed_one, full_query, preferred_element_type=jnp.float32).reshape(
        seq_local, length, heads_local, HEAD_DIM
    )
    key_lin = jnp.dot(normed_one, full_key, preferred_element_type=jnp.float32).reshape(
        seq_local, length, kv_local, HEAD_DIM
    )
    value_rows = (
        jnp.dot(normed_one, full_value, preferred_element_type=jnp.float32)
        .astype(jnp.bfloat16)
        .reshape(seq_local, length, kv_local, HEAD_DIM)
    )
    query_rot = rotate(query_lin, cosine_table, sine_table).astype(jnp.bfloat16)
    key_rot = rotate(key_lin, cosine_table, sine_table).astype(jnp.bfloat16)

    def forward_one(bundle):
        return attend_forward(bundle[0], bundle[1], bundle[2], bundle[3], score_scale)

    mixed_heads, logsum = lax.map(forward_one, (query_rot, key_rot, value_rows, doc_ids))
    mixed_low = mixed_heads.reshape(tok_local, heads_local * HEAD_DIM).astype(jnp.bfloat16)
    attn_partial = jnp.dot(mixed_low, full_out, preferred_element_type=jnp.float32)
    hidden_in = residual + lax.psum(attn_partial.astype(jnp.bfloat16), "mp").astype(jnp.float32)
    normed_two_float, inverse_two = rms_forward(hidden_in, gain_two)
    normed_two = normed_two_float.astype(jnp.bfloat16)
    gate_lin = jnp.dot(normed_two, full_gate, preferred_element_type=jnp.float32)
    up_lin = jnp.dot(normed_two, full_up, preferred_element_type=jnp.float32)
    sig_gate = jax.nn.sigmoid(gate_lin)
    swish_gate = gate_lin * sig_gate
    hidden = (swish_gate * up_lin).astype(jnp.bfloat16)
    mlp_partial = jnp.dot(hidden, full_down, preferred_element_type=jnp.float32)
    output = (
        hidden_in + lax.psum(mlp_partial.astype(jnp.bfloat16), "mp").astype(jnp.float32)
    ).astype(jnp.bfloat16)
    grad_y = cotangent.astype(jnp.float32) * selection.reshape(tok_local, 1).astype(jnp.float32)
    grad_y_low = grad_y.astype(jnp.bfloat16)
    grad_down = jnp.einsum("tf,td->fd", hidden, grad_y_low, preferred_element_type=jnp.float32)
    grad_hidden = jnp.einsum("td,fd->tf", grad_y_low, full_down, preferred_element_type=jnp.float32)
    grad_gate_low = (grad_hidden * up_lin * sig_gate * (1.0 + gate_lin * (1.0 - sig_gate))).astype(
        jnp.bfloat16
    )
    grad_up_low = (grad_hidden * swish_gate).astype(jnp.bfloat16)
    grad_gate_w = jnp.einsum(
        "td,tf->df", normed_two, grad_gate_low, preferred_element_type=jnp.float32
    )
    grad_up_w = jnp.einsum("td,tf->df", normed_two, grad_up_low, preferred_element_type=jnp.float32)
    partial_two = jnp.einsum(
        "tf,df->td", grad_gate_low, full_gate, preferred_element_type=jnp.float32
    ) + jnp.einsum("tf,df->td", grad_up_low, full_up, preferred_element_type=jnp.float32)
    grad_normed_two = lax.psum(partial_two.astype(jnp.bfloat16), "mp").astype(jnp.float32)
    grad_resid_two, gain_grad_two = rms_backward(hidden_in, inverse_two, gain_two, grad_normed_two)
    grad_h = grad_y + grad_resid_two
    grad_h_low = grad_h.astype(jnp.bfloat16)
    grad_out_w = jnp.einsum("tc,td->cd", mixed_low, grad_h_low, preferred_element_type=jnp.float32)
    grad_mixed = jnp.einsum(
        "td,cd->tc", grad_h_low, full_out, preferred_element_type=jnp.float32
    ).astype(jnp.bfloat16)
    grad_mixed = grad_mixed.reshape(seq_local, length, heads_local * HEAD_DIM)

    def backward_one(bundle):
        return attend_backward(
            bundle[0], bundle[1], bundle[2], bundle[3], bundle[4], bundle[5], score_scale
        )

    grad_query_rot, grad_key_rot, grad_values = lax.map(
        backward_one, (query_rot, key_rot, value_rows, doc_ids, logsum, grad_mixed)
    )
    grad_query_lin = (
        rotate(grad_query_rot, cosine_table, -sine_table)
        .reshape(tok_local, heads_local * HEAD_DIM)
        .astype(jnp.bfloat16)
    )
    grad_key_lin = (
        rotate(grad_key_rot, cosine_table, -sine_table)
        .reshape(tok_local, kv_local * HEAD_DIM)
        .astype(jnp.bfloat16)
    )
    grad_value_low = grad_values.reshape(tok_local, kv_local * HEAD_DIM).astype(jnp.bfloat16)
    grad_query_w = jnp.einsum(
        "td,tc->dc", normed_one, grad_query_lin, preferred_element_type=jnp.float32
    )
    grad_key_w = jnp.einsum(
        "td,tc->dc", normed_one, grad_key_lin, preferred_element_type=jnp.float32
    )
    grad_value_w = jnp.einsum(
        "td,tc->dc", normed_one, grad_value_low, preferred_element_type=jnp.float32
    )
    partial_one = (
        jnp.einsum("tc,dc->td", grad_query_lin, full_query, preferred_element_type=jnp.float32)
        + jnp.einsum("tc,dc->td", grad_key_lin, full_key, preferred_element_type=jnp.float32)
        + jnp.einsum("tc,dc->td", grad_value_low, full_value, preferred_element_type=jnp.float32)
    )
    grad_normed_one = lax.psum(partial_one.astype(jnp.bfloat16), "mp").astype(jnp.float32)
    grad_resid_one, gain_grad_one = rms_backward(residual, inverse_one, gain_one, grad_normed_one)
    input_grad = grad_h + grad_resid_one
    (
        shard_query,
        shard_key,
        shard_value,
        shard_out,
        shard_gate,
        shard_up,
        shard_down,
        shard_gain_one,
        shard_gain_two,
    ) = (
        lax.psum_scatter(
            grad_query_w.astype(jnp.bfloat16), "dp", scatter_dimension=0, tiled=True
        ).astype(jnp.float32),
        lax.psum_scatter(
            grad_key_w.astype(jnp.bfloat16), "dp", scatter_dimension=0, tiled=True
        ).astype(jnp.float32),
        lax.psum_scatter(
            grad_value_w.astype(jnp.bfloat16), "dp", scatter_dimension=0, tiled=True
        ).astype(jnp.float32),
        lax.psum_scatter(
            grad_out_w.astype(jnp.bfloat16), "dp", scatter_dimension=1, tiled=True
        ).astype(jnp.float32),
        lax.psum_scatter(
            grad_gate_w.astype(jnp.bfloat16), "dp", scatter_dimension=0, tiled=True
        ).astype(jnp.float32),
        lax.psum_scatter(
            grad_up_w.astype(jnp.bfloat16), "dp", scatter_dimension=0, tiled=True
        ).astype(jnp.float32),
        lax.psum_scatter(
            grad_down.astype(jnp.bfloat16), "dp", scatter_dimension=1, tiled=True
        ).astype(jnp.float32),
        lax.psum_scatter(
            gain_grad_one.astype(jnp.bfloat16), "dp", scatter_dimension=0, tiled=True
        ).astype(jnp.float32),
        lax.psum_scatter(
            gain_grad_two.astype(jnp.bfloat16), "dp", scatter_dimension=0, tiled=True
        ).astype(jnp.float32),
    )
    return (
        output,
        input_grad,
        shard_query,
        shard_key,
        shard_value,
        shard_out,
        shard_gate,
        shard_up,
        shard_down,
        shard_gain_one,
        shard_gain_two,
    )


def solution(mesh):
    in_specs = (
        P("dp", None),
        P("dp", None),
        P("dp", None),
        P("dp", "mp"),
        P("dp", "mp"),
        P("dp", "mp"),
        P("mp", "dp"),
        P("dp", "mp"),
        P("dp", "mp"),
        P("mp", "dp"),
        P("dp"),
        P("dp"),
        P("dp", None),
    )
    out_specs = (
        P("dp", None),
        P("dp", None),
        P("dp", "mp"),
        P("dp", "mp"),
        P("dp", "mp"),
        P("mp", "dp"),
        P("dp", "mp"),
        P("dp", "mp"),
        P("mp", "dp"),
        P("dp"),
        P("dp"),
    )
    return jax.shard_map(
        per_device, mesh=mesh, in_specs=in_specs, out_specs=out_specs, check_vma=False
    )
```

profile of v0, /device:TPU:0, one launch (start us, length us, event | category | flops | bytes accessed | tf_op | source)
XLA Modules:
  0.0 1349.3 jit_solution(685220449423602048)
XLA Ops:
  68.6 15.0 %while.26 = (s32[]{:T(128)}, bf16[2,512,512]{2,1,0:T(8,128)(2,1)S(1)}, f32[2,1,8,512,1]{3,2,4,1,0:T(8,128)}, bf16[2,512,1,64]{1,3,2,0:T(8,128)(2,1)S(1)}, s32[2,...) while((s32[]{:T(128)}, ...), condition=%wide.region_4.5_spmd, body=%wide.region_1.4_spmd.sunk | while | flops 562819072 | bytes 29629548 | solution.py:164
  100.7 144.7 %all-reduce.8.cloned.1.call-done = bf16[1024,2048]{1,0:T(8,128)(2,1)} async-done(((bf16[1024,2048]{1,0:T(8,128)(2,1)}), bf16[1024,2048]{1,0:T(8,128)(2,1)}) %all-reduce.8.cloned.1.call-update) | async-done | bytes 4194320 | tf_op jit(solution)/shard_map/psum | solution.py:167
  255.4 34.0 %all-gather.14.cloned.1.call-done = bf16[2048,1408]{1,0:T(8,128)(2,1)} async-done(((bf16[256,1408]{1,0:T(8,128)(2,1)}), bf16[2048,1408]{1,0:T(8,128)(2,1)}) %all-gather.14.cloned.1.call-update) | async-done | bytes 5767184 | tf_op jit(solution)/shard_map/all_gather | solution.py:131
  289.3 11.7 fusion.91
  301.0 33.3 %all-gather.12.cloned.1.call-done = bf16[2048,1408]{1,0:T(8,128)(2,1)} async-done(((bf16[256,1408]{1,0:T(8,128)(2,1)}), bf16[2048,1408]{1,0:T(8,128)(2,1)}) %all-gather.12.cloned.1.call-update) | async-done | bytes 5767184 | tf_op jit(solution)/shard_map/all_gather | solution.py:130
  334.3 11.7 fusion.90
  346.0 34.3 %all-gather.16.cloned.1.call-done = bf16[1408,2048]{1,0:T(8,128)(2,1)} async-done(((bf16[1408,256]{1,0:T(8,128)(2,1)}), bf16[1408,2048]{1,0:T(8,128)(2,1)}) %all-gather.16.cloned.1.call-update) | async-done | bytes 5767184 | tf_op jit(solution)/shard_map/all_gather | solution.py:132
  380.3 17.0 %multiply_convert_fusion.1 = (bf16[1024,1408]{1,0:T(8,128)(2,1)}, bf16[1024,1408]{1,0:T(8,128)(2,1)}, bf16[1024,1408]{1,0:T(8,128)(2,1)}) fusion(f32[1024,1408]{1,0:T(8,128)} %fusion.90, f32[1024,1408]{1,0:T(8,128)} %fusion.91, bf16[1408,2048]{1,0:T(8,128)(2,1)} %all-gather.16.cloned.1.call-done, bf16[1024,2048]{1,0:T(8,128)(2,1)} %param.29, ...), kind=kOutput, calls=%fused_computation.103 | convolution fusion | flops 5933498368 | bytes 30150656 | tf_op jit(solution)/shard_map/td,fd->tf/dot_general | solution.py:182
  406.0 11.0 add_convert_fusion.1
  417.1 155.1 %all-reduce.10.cloned.1.call-done = bf16[1024,2048]{1,0:T(8,128)(2,1)} async-done(((bf16[1024,2048]{1,0:T(8,128)(2,1)}), bf16[1024,2048]{1,0:T(8,128)(2,1)}) %all-reduce.10.cloned.1.call-update) | async-done | bytes 4194320 | tf_op jit(solution)/shard_map/psum | solution.py:194
  590.2 70.1 %while.27 = (s32[]{:T(128)}, f32[2,512,8,64]{1,0,3,2:T(2,128)}, f32[2,512,1,64]{1,3,2,0:T(8,128)}, bf16[2,512,1,64]{1,3,2,0:T(8,128)(2,1)}, bf16[2,512,1,64]{1,3...) while((s32[]{:T(128)}, f32[2,512,8,64]{1,0,3,2:T(2,128)}, ...), condition=%wide.region_12.13_spmd, body=%wide.region_10.12_spmd.sunk | while | flops 1374711808 | bytes 77127944 | solution.py:209
  605.9 19.6 %dynamic_update_slice.32 = f32[2,512,8,64]{1,0,3,2:T(2,128)} dynamic-update-slice(f32[2,512,8,64]{1,0,3,2:T(2,128)} %get-tuple-element.378, f32[1,512,8,64]{1,0,3,2:T(1,128)S(1)} %copy.100, s32[]{:T(128)S(6)} %copy.121, s32[]{:T(128)} %constant.66.clone.1..sunk, s32[]{:T(128)} %constant.66.clone.1..sunk, s32[]{:T(128)} %constant.66.clone.1..sunk) | dynamic-update-slice | bytes 2097156 | tf_op jit(solution)/shard_map/while/body/jit(dynamic_update_index_in_dim)/dynamic_update_slice | solution.py:209
  640.7 19.6 %dynamic_update_slice.32 = f32[2,512,8,64]{1,0,3,2:T(2,128)} dynamic-update-slice(f32[2,512,8,64]{1,0,3,2:T(2,128)} %get-tuple-element.378, f32[1,512,8,64]{1,0,3,2:T(1,128)S(1)} %copy.100, s32[]{:T(128)S(6)} %copy.121, s32[]{:T(128)} %constant.66.clone.1..sunk, s32[]{:T(128)} %constant.66.clone.1..sunk, s32[]{:T(128)} %constant.66.clone.1..sunk) | dynamic-update-slice | bytes 2097156 | tf_op jit(solution)/shard_map/while/body/jit(dynamic_update_index_in_dim)/dynamic_update_slice | solution.py:209
  688.0 11.0 convolution_convert_fusion.1
  699.1 11.0 convolution_convert_fusion.2
  721.9 10.9 convolution_convert_fusion.3
  744.7 37.6 %reduce-scatter.8.cloned.1.call-done = bf16[256,512]{1,0:T(8,128)(2,1)} async-done(((bf16[2048,512]{1,0:T(8,128)(2,1)}), bf16[256,512]{1,0:T(8,128)(2,1)}) %reduce-scatter.8.cloned.1.call-update) | async-done | bytes 262160 | tf_op jit(solution)/shard_map/reduce_scatter | solution.py:251
  784.1 42.6 %reduce-scatter.14.cloned.1.call-done = bf16[512,256]{1,0:T(8,128)(2,1)} async-done(((bf16[512,2048]{1,0:T(8,128)(2,1)}), bf16[512,256]{1,0:T(8,128)(2,1)}) %reduce-scatter.14.cloned.1.call-update) | async-done | bytes 262160 | tf_op jit(solution)/shard_map/reduce_scatter | solution.py:260
  828.6 60.6 %reduce-scatter.18.cloned.1.call-done = bf16[256,1408]{1,0:T(8,128)(2,1)} async-done(((bf16[2048,1408]{1,0:T(8,128)(2,1)}), bf16[256,1408]{1,0:T(8,128)(2,1)}) %reduce-scatter.18.cloned.1.call-update) | async-done | bytes 720912 | tf_op jit(solution)/shard_map/reduce_scatter | solution.py:266
  891.4 60.2 %reduce-scatter.16.cloned.1.call-done = bf16[256,1408]{1,0:T(8,128)(2,1)} async-done(((bf16[2048,1408]{1,0:T(8,128)(2,1)}), bf16[256,1408]{1,0:T(8,128)(2,1)}) %reduce-scatter.16.cloned.1.call-update) | async-done | bytes 720912 | tf_op jit(solution)/shard_map/reduce_scatter | solution.py:263
  954.0 59.9 %reduce-scatter.20.cloned.1.call-done = bf16[1408,256]{1,0:T(8,128)(2,1)} async-done(((bf16[1408,2048]{1,0:T(8,128)(2,1)}), bf16[1408,256]{1,0:T(8,128)(2,1)}) %reduce-scatter.20.cloned.1.call-update) | async-done | bytes 720912 | tf_op jit(solution)/shard_map/reduce_scatter | solution.py:269
  1016.2 291.6 %all-reduce.12.cloned.1.call-done = (bf16[1024,2048]{1,0:T(8,128)(2,1)}, bf16[1024,2048]{1,0:T(8,128)(2,1)}) async-done(((bf16[1024,2048]{1,0:T(8,128)(2,1)}, bf16[1024,2048]{1,0:T(8,128)(2,1)}), (bf16[1024,2048]{1,0:T(8,128)(2,1)}, bf16[1024,2048]{1,0:T(8,128)(2,1)})) %all-reduce.12.cloned.1.call-update) | async-done | bytes 8388624 | tf_op jit(solution)/shard_map/psum | solution.py:177
  1313.4 13.7 %all-reduce.2 = (bf16[2048]{0:T(1024)(128)(2,1)S(1)}, bf16[2048]{0:T(1024)(128)(2,1)S(1)}) all-reduce(bf16[2048]{0:T(1024)(128)(2,1)S(1)} %get-tuple-element.161, bf16[2048]{0:T(1024)(128)(2,1)S(1)} %copy-done.24), channel_id=9, replica_groups=mesh['dp'=8,'mp'=4] {'dp'}, use_global_device_ids=true, to_apply=%region_23.24.clone | all-reduce | flops 4096 | bytes 16384
  1327.8 14.6 %fusion.60 = (f32[1024,2048]{1,0:T(8,128)}, bf16[1024,2048]{1,0:T(8,128)(2,1)}) fusion(f32[1024,2048]{1,0:T(8,128)} %copy-done.6, bf16[1024,2048]{1,0:T(8,128)(2,1)} %get-tuple-element.200, bf16[1024,2048]{1,0:T(8,128)(2,1)} %param.17, f32[1024]{0:T(1024)S(1)} %broadcast_multiply_fusion, f32[1024]{0:T(1024)S(1)} %copy-done.23, f32[2048]{0:T(1024)S(1)} %bitcast.299, ...), kind=kLoop, calls=%fused_computation.80 | loop fusion | flops 27262976 | bytes 37769216 | tf_op jit(solution)/shard_map/add | solution.py:239
  (220 shorter events, 227.5 us)
Async XLA Ops:
  7.2 46.4 %all-gather.8.cloned.1.call-start = ((), (), s32[]{:S(2)}) async-start(), calls=%async_computation.7 | async-start | bytes 2359296 | tf_op jit(solution)/shard_map/all_gather | solution.py:126
  7.9 75.8 %all-gather.10.cloned.1.call-start = ((), (), s32[]{:S(2)}) async-start(), calls=%async_computation.8 | async-start | bytes 2359296 | tf_op jit(solution)/shard_map/all_gather | solution.py:129
  8.7 236.7 %all-reduce.8.cloned.1.call-start = ((), (), s32[]{:S(2)}) async-start(), calls=%async_computation.9 | async-start | bytes 8388608 | tf_op jit(solution)/shard_map/psum | solution.py:167
  8.7 36.2 %copy-start = (bf16[1024,2048]{1,0:T(8,128)(2,1)S(1)}, bf16[1024,2048]{1,0:T(8,128)(2,1)}, u32[]{:S(2)}) copy-start(bf16[1024,2048]{1,0:T(8,128)(2,1)} %param.17) | copy-start | bytes 12582916
  13.4 32.6 %copy-start.21 = (f32[1024]{0:T(1024)}, f32[1024]{0:T(1024)S(1)}, u32[]{:S(2)}) copy-start(f32[1024]{0:T(1024)S(1)} %get-tuple-element.221) | copy-start | bytes 12292
  23.8 22.1 %copy-start.19 = (f32[8,1,256]{2,1,0:T(1,128)}, f32[8,1,256]{2,1,0:T(1,128)S(1)}, u32[]{:S(2)}) copy-start(f32[8,1,256]{2,1,0:T(1,128)S(1)} %convert_element_type.218) | copy-start | bytes 24580
  24.8 39.6 %copy-start.12 = (f32[512,32]{0,1:T(8,128)}, f32[512,32]{0,1:T(8,128)S(1)}, u32[]{:S(2)}) copy-start(f32[512,32]{0,1:T(8,128)S(1)} %get-tuple-element.226) | copy-start | bytes 196612
  90.1 199.3 %all-gather.14.cloned.1.call-start = ((), (), s32[]{:S(2)}) async-start(), calls=%async_computation.11 | async-start | bytes 6488064 | tf_op jit(solution)/shard_map/all_gather | solution.py:131
  90.6 243.6 %all-gather.12.cloned.1.call-start = ((), (), s32[]{:S(2)}) async-start(), calls=%async_computation.10 | async-start | bytes 6488064 | tf_op jit(solution)/shard_map/all_gather | solution.py:130
  91.2 289.1 %all-gather.16.cloned.1.call-start = ((), (), s32[]{:S(2)}) async-start(), calls=%async_computation.12 | async-start | bytes 6488064 | tf_op jit(solution)/shard_map/all_gather | solution.py:132
  91.8 480.3 %all-reduce.10.cloned.1.call-start = ((), (), s32[]{:S(2)}) async-start(), calls=%async_computation.13 | async-start | bytes 8388608 | tf_op jit(solution)/shard_map/psum | solution.py:194
  91.9 488.8 %copy-start.25 = (f32[1,4,2,128]{3,1,2,0:T(4,128)}, f32[1,4,2,128]{3,1,2,0:T(4,128)S(1)}, u32[]{:S(2)}) copy-start(f32[1,4,2,128]{3,1,2,0:T(4,128)S(1)} %copy.87) | copy-start | bytes 12292
  417.0 324.9 %reduce-scatter.10.cloned.1.call-start = ((), (), s32[]{:S(2)}) async-start(), calls=%async_computation.15 | async-start | bytes 294912 | tf_op jit(solution)/shard_map/reduce_scatter | solution.py:254
  668.0 75.3 %reduce-scatter.12.cloned.1.call-start = ((), (), s32[]{:S(2)}) async-start(), calls=%async_computation.16 | async-start | bytes 294912 | tf_op jit(solution)/shard_map/reduce_scatter | solution.py:257
  674.7 107.7 %reduce-scatter.8.cloned.1.call-start = ((), (), s32[]{:S(2)}) async-start(), calls=%async_computation.14 | async-start | bytes 2359296 | tf_op jit(solution)/shard_map/reduce_scatter | solution.py:251
  680.8 146.0 %reduce-scatter.14.cloned.1.call-start = ((), (), s32[]{:S(2)}) async-start(), calls=%async_computation.17 | async-start | bytes 2359296 | tf_op jit(solution)/shard_map/reduce_scatter | solution.py:260
  687.9 201.2 %reduce-scatter.18.cloned.1.call-start = ((), (), s32[]{:S(2)}) async-start(), calls=%async_computation.19 | async-start | bytes 6488064 | tf_op jit(solution)/shard_map/reduce_scatter | solution.py:266
  699.0 252.6 %reduce-scatter.16.cloned.1.call-start = ((), (), s32[]{:S(2)}) async-start(), calls=%async_computation.18 | async-start | bytes 6488064 | tf_op jit(solution)/shard_map/reduce_scatter | solution.py:263
  710.1 303.8 %reduce-scatter.20.cloned.1.call-start = ((), (), s32[]{:S(2)}) async-start(), calls=%async_computation.20 | async-start | bytes 6488064 | tf_op jit(solution)/shard_map/reduce_scatter | solution.py:269
  721.6 586.1 %all-reduce.12.cloned.1.call-start = ((), (), s32[]{:S(2)}) async-start(), calls=%async_computation.21 | async-start | bytes 16777216 | tf_op jit(solution)/shard_map/psum | solution.py:177
  740.0 567.7 %copy-start.20 = (f32[8,1,256]{2,1,0:T(1,128)S(1)}, f32[8,1,256]{2,1,0:T(1,128)}, u32[]{:S(2)}) copy-start(f32[8,1,256]{2,1,0:T(1,128)} %copy-done.19) | copy-start | bytes 24580
  740.0 567.7 %copy-start.22 = (f32[1024]{0:T(1024)S(1)}, f32[1024]{0:T(1024)}, u32[]{:S(2)}) copy-start(f32[1024]{0:T(1024)} %copy-done.21) | copy-start | bytes 12292
  953.9 359.5 %copy-start.24 = (bf16[2048]{0:T(1024)(128)(2,1)S(1)}, bf16[2048]{0:T(1024)(128)(2,1)}, u32[]{:S(2)}) copy-start(bf16[2048]{0:T(1024)(128)(2,1)} %get-tuple-element.159) | copy-start | bytes 12292
  953.9 373.8 %copy-start.23 = (f32[1024]{0:T(1024)S(1)}, f32[1024]{0:T(1024)}, u32[]{:S(2)}) copy-start(f32[1024]{0:T(1024)} %get-tuple-element.220) | copy-start | bytes 12292
  (29 other events, 139.6 us)
Sparse Core Ops, SparseCore 0:
  9.9 30.9 all-gather.7
  42.7 28.2 all-gather.9
  90.2 155.1 all-reduce.7
  247.1 42.1 all-gather.13
  291.0 43.1 all-gather.11
  336.0 44.2 all-gather.15
  417.1 154.9 all-reduce.9
  668.1 32.6 reduce-scatter.9
  704.4 33.6 reduce-scatter.11
  741.2 41.0 reduce-scatter.7
  785.6 41.1 reduce-scatter.13
  830.1 59.0 reduce-scatter.17
  892.6 59.0 reduce-scatter.15
  954.9 58.8 reduce-scatter.19
  1016.9 290.8 all-reduce.11
where the time goes:
time: 1360 us; the launch traced here: 1350 us
  waiting for transfers between devices  957 us (70%)
  matrix products  177 us (13%)
  other arithmetic  83.6 us (6%)
  local copies, waits for them, and re-layouts  61.2 us (4%)
  blocking collectives  53 us (4%)
  between operations  15.5 us (1%)
    psum x1, waiting for transfers between devices, per_device(): lax.psum(mlp_partial.astype(jnp.bfloat16), 'mp').astype(jnp.float32)  292 us
    psum x1, waiting for transfers between devices, per_device(): lax.psum(partial_two.astype(jnp.bfloat16), 'mp').astype(jnp.float32)  155 us
    psum x1, waiting for transfers between devices, per_device(): lax.psum(attn_partial.astype(jnp.bfloat16), 'mp').astype(jnp.float32)  145 us
    reduce_scatter x1, waiting for transfers between devices, per_device(): lax.psum_scatter(grad_up_w.astype(jnp.bfloat16), 'dp', scatter_dimension=...  60.6 us
    reduce_scatter x1, waiting for transfers between devices, per_device(): lax.psum_scatter(grad_gate_w.astype(jnp.bfloat16), 'dp', scatter_dimensio...  60.2 us
    reduce_scatter x1, waiting for transfers between devices, per_device(): lax.psum_scatter(grad_down.astype(jnp.bfloat16), 'dp', scatter_dimension=...  59.9 us
    reduce_scatter x1, waiting for transfers between devices, per_device(): lax.psum_scatter(grad_out_w.astype(jnp.bfloat16), 'dp', scatter_dimension...  42.6 us
    dynamic_update_slice x4, local copies, waits for them, and re-layouts, per_device(): lax.map(backward_one, (query_rot, key_rot, value_rows, doc_ids, logsum, g...  41.4 us
  transfers between devices with their start and end apart: 15, of which 11 were waited for; matrix products, arithmetic and copies ran while one was open for 12% of the time, Pallas kernels for 0%

commit v1 on v0

--- a/solution.py
+++ b/solution.py
@@ -6,6 +6,22 @@
 HEAD_DIM = 64
 EPSILON = 1e-05
 MASKED = -1e30
+
+
+def ring_gather(x, axis, dim):
+    ways, here, step = (lax.axis_size(axis), lax.axis_index(axis), x.shape[dim])
+    shape = [n * ways if d == dim else n for d, n in enumerate(x.shape)]
+    full = lax.dynamic_update_slice_in_dim(jnp.zeros(shape, x.dtype), x, here * step, axis=dim)
+    going_up = going_down = x
+    for far in range(1, ways // 2 + 1):
+        going_up = lax.ppermute(going_up, axis, [(d, (d + 1) % ways) for d in range(ways)])
+        full = lax.dynamic_update_slice_in_dim(full, going_up, (here - far) % ways * step, axis=dim)
+        if 2 * far < ways:
+            going_down = lax.ppermute(going_down, axis, [(d, (d - 1) % ways) for d in range(ways)])
+            full = lax.dynamic_update_slice_in_dim(
+                full, going_down, (here + far) % ways * step, axis=dim
+            )
+    return full
 
 
 def rope_tables(length, head_width):
@@ -129,7 +145,7 @@
         lax.all_gather(w_out, "dp", axis=1, tiled=True),
         lax.all_gather(w_gate, "dp", axis=0, tiled=True),
         lax.all_gather(w_up, "dp", axis=0, tiled=True),
-        lax.all_gather(w_down, "dp", axis=1, tiled=True),
+        ring_gather(w_down, "dp", 1),
         lax.all_gather(attn_gain, "dp", axis=0, tiled=True),
         lax.all_gather(mlp_gain, "dp", axis=0, tiled=True),
     )

time: 1360 us -> 1320 us (0.971)
  waiting for transfers between devices: 957 us -> 898 us
    psum x1, waiting for transfers between devices: 145 us -> 86.4 us  [per_device(): lax.psum(attn_partial.astype(jnp.bfloat16), 'mp').astype(jnp.float32)]
    all_gather x1 -> x0, waiting for transfers between devices: 34.3 us -> none  [per_device(): lax.all_gather(w_down, 'dp', axis=1, tiled=True)]
    ppermute x0 -> x7, waiting for transfers between devices: none -> 33.5 us  [the longest x4 18.2 us: ring_gather(): lax.ppermute(going_up, axis, [(d, (d + 1) % ways) for d in range(ways)])]
  transfers between devices with their start and end apart: 15 -> 21, of which waited for: 11 -> 14; matrix products, arithmetic and copies ran while one was open for 12% -> 12% of each run, Pallas kernels for 0% -> 0%
where the time goes in v1:
time: 1320 us; the launch traced here: 1310 us
  waiting for transfers between devices  898 us (68%)
  matrix products  177 us (13%)
  other arithmetic  83.5 us (6%)
  local copies, waits for them, and re-layouts  74.8 us (6%)
  blocking collectives  56.8 us (4%)
  between operations  15.6 us (1%)
    psum x1, waiting for transfers between devices, per_device(): lax.psum(mlp_partial.astype(jnp.bfloat16), 'mp').astype(jnp.float32)  292 us
    psum x1, waiting for transfers between devices, per_device(): lax.psum(partial_two.astype(jnp.bfloat16), 'mp').astype(jnp.float32)  155 us
    psum x1, waiting for transfers between devices, per_device(): lax.psum(attn_partial.astype(jnp.bfloat16), 'mp').astype(jnp.float32)  86.4 us
    reduce_scatter x1, waiting for transfers between devices, per_device(): lax.psum_scatter(grad_up_w.astype(jnp.bfloat16), 'dp', scatter_dimension=...  60.7 us
    reduce_scatter x1, waiting for transfers between devices, per_device(): lax.psum_scatter(grad_gate_w.astype(jnp.bfloat16), 'dp', scatter_dimensio...  60.1 us
    reduce_scatter x1, waiting for transfers between devices, per_device(): lax.psum_scatter(grad_down.astype(jnp.bfloat16), 'dp', scatter_dimension=...  60 us
    reduce_scatter x1, waiting for transfers between devices, per_device(): lax.psum_scatter(grad_out_w.astype(jnp.bfloat16), 'dp', scatter_dimension...  42.5 us
    dynamic_update_slice x4, local copies, waits for them, and re-layouts, per_device(): lax.map(backward_one, (query_rot, key_rot, value_rows, doc_ids, logsum, g...  41.2 us
  transfers between devices with their start and end apart: 21, of which 14 were waited for; matrix products, arithmetic and copies ran while one was open for 12% of the time, Pallas kernels for 0%

profile of v1, /device:TPU:0, one launch (start us, length us, event | category | flops | bytes accessed | tf_op | source)
XLA Modules:
  0.0 1314.6 jit_solution(2002294873746499841)
XLA Ops:
  69.1 15.1 %while.26 = (s32[]{:T(128)}, bf16[2,512,512]{2,1,0:T(8,128)(2,1)S(1)}, f32[2,1,8,512,1]{3,2,4,1,0:T(8,128)}, bf16[2,512,1,64]{1,3,2,0:T(8,128)(2,1)S(1)}, s32[2,...) while((s32[]{:T(128)}, ...), condition=%wide.region_4.5_spmd, body=%wide.region_1.4_spmd.sunk | while | flops 562819072 | bytes 29629548 | solution.py:180
  94.5 16.2 %collective-permute-done = bf16[1408,256]{1,0:T(8,128)(2,1)} collective-permute-done((bf16[1408,256]{1,0:T(8,128)(2,1)S(1)}, bf16[1408,256]{1,0:T(8,128)(2,1)}, u32[]{:S(2)}, u32[]{:S(2)}) %collective-permute-start) | collective-permute-done | bytes 720928 | tf_op jit(solution)/shard_map/ppermute | solution.py:17
  110.7 12.5 all-gather.1
  159.3 86.4 %all-reduce.8.cloned.1.call-done = bf16[1024,2048]{1,0:T(8,128)(2,1)} async-done(((bf16[1024,2048]{1,0:T(8,128)(2,1)}), bf16[1024,2048]{1,0:T(8,128)(2,1)}) %all-reduce.8.cloned.1.call-update) | async-done | bytes 4194320 | tf_op jit(solution)/shard_map/psum | solution.py:183
  255.6 34.0 %all-gather.13.cloned.1.call-done = bf16[2048,1408]{1,0:T(8,128)(2,1)} async-done(((bf16[256,1408]{1,0:T(8,128)(2,1)}), bf16[2048,1408]{1,0:T(8,128)(2,1)}) %all-gather.13.cloned.1.call-update) | async-done | bytes 5767184 | tf_op jit(solution)/shard_map/all_gather | solution.py:147
  289.6 11.7 fusion.91
  301.3 33.3 %all-gather.11.cloned.1.call-done = bf16[2048,1408]{1,0:T(8,128)(2,1)} async-done(((bf16[256,1408]{1,0:T(8,128)(2,1)}), bf16[2048,1408]{1,0:T(8,128)(2,1)}) %all-gather.11.cloned.1.call-update) | async-done | bytes 5767184 | tf_op jit(solution)/shard_map/all_gather | solution.py:146
  334.6 11.8 fusion.90
  346.4 14.9 %multiply_convert_fusion.1 = (bf16[1024,1408]{1,0:T(8,128)(2,1)}, bf16[1024,1408]{1,0:T(8,128)(2,1)S(1)}, bf16[1024,1408]{1,0:T(8,128)(2,1)}) fusion(f32[1024,1408]{1,0:T(8,128)} %fusion.90, f32[1024,1408]{1,0:T(8,128)} %fusion.91, bf16[1408,2048]{1,0:T(8,128)(2,1)} %constant_dynamic-update-slice_fusion.1, bf16[1024,2048]{1,0:T(8,128)(2,1)S(1)} %copy-done.8, ...), kind=kOutput, calls=%fused_computation.103 | convolution fusion | flops 5933498368 | bytes 30150656 | tf_op jit(solution)/shard_map/td,fd->tf/dot_general | solution.py:198
  371.1 11.2 add_convert_fusion.1
  382.4 155.0 %all-reduce.10.cloned.1.call-done = bf16[1024,2048]{1,0:T(8,128)(2,1)} async-done(((bf16[1024,2048]{1,0:T(8,128)(2,1)}), bf16[1024,2048]{1,0:T(8,128)(2,1)}) %all-reduce.10.cloned.1.call-update) | async-done | bytes 4194320 | tf_op jit(solution)/shard_map/psum | solution.py:210
  555.5 70.0 %while.27 = (s32[]{:T(128)}, f32[2,512,8,64]{1,0,3,2:T(2,128)}, f32[2,512,1,64]{1,3,2,0:T(8,128)}, bf16[2,512,1,64]{1,3,2,0:T(8,128)(2,1)}, bf16[2,512,1,64]{1,3...) while((s32[]{:T(128)}, f32[2,512,8,64]{1,0,3,2:T(2,128)}, ...), condition=%wide.region_12.13_spmd, body=%wide.region_10.12_spmd.sunk | while | flops 1374711808 | bytes 77127944 | solution.py:225
  571.2 19.5 %dynamic_update_slice.72 = f32[2,512,8,64]{1,0,3,2:T(2,128)} dynamic-update-slice(f32[2,512,8,64]{1,0,3,2:T(2,128)} %get-tuple-element.378, f32[1,512,8,64]{1,0,3,2:T(1,128)S(1)} %copy.100, s32[]{:T(128)S(6)} %copy.129, s32[]{:T(128)} %constant.115.clone.1..sunk, s32[]{:T(128)} %constant.115.clone.1..sunk, s32[]{:T(128)} %constant.115.clone.1..sunk) | dynamic-update-slice | bytes 2097156 | tf_op jit(solution)/shard_map/while/body/jit(dynamic_update_index_in_dim)/dynamic_update_slice | solution.py:225
  606.0 19.5 %dynamic_update_slice.72 = f32[2,512,8,64]{1,0,3,2:T(2,128)} dynamic-update-slice(f32[2,512,8,64]{1,0,3,2:T(2,128)} %get-tuple-element.378, f32[1,512,8,64]{1,0,3,2:T(1,128)S(1)} %copy.100, s32[]{:T(128)S(6)} %copy.129, s32[]{:T(128)} %constant.115.clone.1..sunk, s32[]{:T(128)} %constant.115.clone.1..sunk, s32[]{:T(128)} %constant.115.clone.1..sunk) | dynamic-update-slice | bytes 2097156 | tf_op jit(solution)/shard_map/while/body/jit(dynamic_update_index_in_dim)/dynamic_update_slice | solution.py:225
  653.2 11.0 convolution_convert_fusion.1
  664.3 11.0 convolution_convert_fusion.2
  710.0 37.7 %reduce-scatter.8.cloned.1.call-done = bf16[256,512]{1,0:T(8,128)(2,1)} async-done(((bf16[2048,512]{1,0:T(8,128)(2,1)}), bf16[256,512]{1,0:T(8,128)(2,1)}) %reduce-scatter.8.cloned.1.call-update) | async-done | bytes 262160 | tf_op jit(solution)/shard_map/reduce_scatter | solution.py:267
  749.5 42.5 %reduce-scatter.14.cloned.1.call-done = bf16[512,256]{1,0:T(8,128)(2,1)} async-done(((bf16[512,2048]{1,0:T(8,128)(2,1)}), bf16[512,256]{1,0:T(8,128)(2,1)}) %reduce-scatter.14.cloned.1.call-update) | async-done | bytes 262160 | tf_op jit(solution)/shard_map/reduce_scatter | solution.py:276
  793.7 60.7 %reduce-scatter.18.cloned.1.call-done = bf16[256,1408]{1,0:T(8,128)(2,1)} async-done(((bf16[2048,1408]{1,0:T(8,128)(2,1)}), bf16[256,1408]{1,0:T(8,128)(2,1)}) %reduce-scatter.18.cloned.1.call-update) | async-done | bytes 720912 | tf_op jit(solution)/shard_map/reduce_scatter | solution.py:282
  856.8 60.1 %reduce-scatter.16.cloned.1.call-done = bf16[256,1408]{1,0:T(8,128)(2,1)} async-done(((bf16[2048,1408]{1,0:T(8,128)(2,1)}), bf16[256,1408]{1,0:T(8,128)(2,1)}) %reduce-scatter.16.cloned.1.call-update) | async-done | bytes 720912 | tf_op jit(solution)/shard_map/reduce_scatter | solution.py:279
  919.1 60.0 %reduce-scatter.20.cloned.1.call-done = bf16[1408,256]{1,0:T(8,128)(2,1)} async-done(((bf16[1408,2048]{1,0:T(8,128)(2,1)}), bf16[1408,256]{1,0:T(8,128)(2,1)}) %reduce-scatter.20.cloned.1.call-update) | async-done | bytes 720912 | tf_op jit(solution)/shard_map/reduce_scatter | solution.py:285
  981.5 291.6 %all-reduce.12.cloned.1.call-done = (bf16[1024,2048]{1,0:T(8,128)(2,1)}, bf16[1024,2048]{1,0:T(8,128)(2,1)}) async-done(((bf16[1024,2048]{1,0:T(8,128)(2,1)}, bf16[1024,2048]{1,0:T(8,128)(2,1)}), (bf16[1024,2048]{1,0:T(8,128)(2,1)}, bf16[1024,2048]{1,0:T(8,128)(2,1)})) %all-reduce.12.cloned.1.call-update) | async-done | bytes 8388624 | tf_op jit(solution)/shard_map/psum | solution.py:193
  1278.8 13.7 %all-reduce.2 = (bf16[2048]{0:T(1024)(128)(2,1)S(1)}, bf16[2048]{0:T(1024)(128)(2,1)S(1)}) all-reduce(bf16[2048]{0:T(1024)(128)(2,1)S(1)} %get-tuple-element.161, bf16[2048]{0:T(1024)(128)(2,1)S(1)} %copy-done.28), channel_id=9, replica_groups=mesh['dp'=8,'mp'=4] {'dp'}, use_global_device_ids=true, to_apply=%region_23.24.clone | all-reduce | flops 4096 | bytes 16384
  1293.1 14.6 %fusion.60 = (f32[1024,2048]{1,0:T(8,128)}, bf16[1024,2048]{1,0:T(8,128)(2,1)}) fusion(f32[1024,2048]{1,0:T(8,128)} %copy-done.6, bf16[1024,2048]{1,0:T(8,128)(2,1)} %get-tuple-element.200, bf16[1024,2048]{1,0:T(8,128)(2,1)} %param.17, f32[1024]{0:T(1024)S(1)} %broadcast_multiply_fusion, f32[1024]{0:T(1024)S(1)} %copy-done.25, f32[2048]{0:T(1024)S(1)} %bitcast.299, ...), kind=kLoop, calls=%fused_computation.80 | loop fusion | flops 27262976 | bytes 37769216 | tf_op jit(solution)/shard_map/add | solution.py:255
  (244 shorter events, 269.4 us)
Async XLA Ops:
  7.2 46.4 %all-gather.7.cloned.1.call-start = ((), (), s32[]{:S(2)}) async-start(), calls=%async_computation.7 | async-start | bytes 2359296 | tf_op jit(solution)/shard_map/all_gather | solution.py:142
  7.9 76.3 %all-gather.9.cloned.1.call-start = ((), (), s32[]{:S(2)}) async-start(), calls=%async_computation.8 | async-start | bytes 2359296 | tf_op jit(solution)/shard_map/all_gather | solution.py:145
  8.7 237.0 %all-reduce.8.cloned.1.call-start = ((), (), s32[]{:S(2)}) async-start(), calls=%async_computation.9 | async-start | bytes 8388608 | tf_op jit(solution)/shard_map/psum | solution.py:183
  90.5 199.1 %all-gather.13.cloned.1.call-start = ((), (), s32[]{:S(2)}) async-start(), calls=%async_computation.11 | async-start | bytes 6488064 | tf_op jit(solution)/shard_map/all_gather | solution.py:147
  91.1 243.5 %all-gather.11.cloned.1.call-start = ((), (), s32[]{:S(2)}) async-start(), calls=%async_computation.10 | async-start | bytes 6488064 | tf_op jit(solution)/shard_map/all_gather | solution.py:146
  91.7 445.8 %all-reduce.10.cloned.1.call-start = ((), (), s32[]{:S(2)}) async-start(), calls=%async_computation.12 | async-start | bytes 8388608 | tf_op jit(solution)/shard_map/psum | solution.py:210
  91.8 18.9 %collective-permute-start = (bf16[1408,256]{1,0:T(8,128)(2,1)S(1)}, bf16[1408,256]{1,0:T(8,128)(2,1)}, u32[]{:S(2)}, u32[]{:S(2)}) collective-permute-start(bf16[1408,256]{1,0:T(8,128)(2,1)S(1)} %copy-done.18), channel_id=1, source_target_pairs={{0,4},{4,8},{8,12},{12,16},{16,20},{20,24},{24,28},{28,0},{1,5},{5... | collective-permute-start | bytes 2162696 | tf_op jit(solution)/shard_map/ppermute | solution.py:17
  92.1 31.1 %collective-permute-start.1 = (bf16[1408,256]{1,0:T(8,128)(2,1)S(1)}, bf16[1408,256]{1,0:T(8,128)(2,1)}, u32[]{:S(2)}, u32[]{:S(2)}) collective-permute-start(bf16[1408,256]{1,0:T(8,128)(2,1)S(1)} %copy-done.18), channel_id=1, source_target_pairs={{0,28},{4,0},{8,4},{12,8},{16,12},{20,16},{24,20},{28,24},{1,29},{... | collective-permute-start | bytes 2162696 | tf_op jit(solution)/shard_map/ppermute | solution.py:20
  110.6 19.1 %collective-permute-start.2 = (bf16[1408,256]{1,0:T(8,128)(2,1)}, bf16[1408,256]{1,0:T(8,128)(2,1)S(1)}, u32[]{:S(2)}, u32[]{:S(2)}) collective-permute-start(bf16[1408,256]{1,0:T(8,128)(2,1)} %collective-permute-done), channel_id=1, source_target_pairs={{0,4},{4,8},{8,12},{12,16},{16,20},{20,24},{24,28},{28,0},{1,5},{5... | collective-permute-start | bytes 2162696 | tf_op jit(solution)/shard_map/ppermute | solution.py:17
  110.7 435.3 %copy-start.26 = (f32[1,4,2,128]{3,1,2,0:T(4,128)}, f32[1,4,2,128]{3,1,2,0:T(4,128)S(1)}, u32[]{:S(2)}) copy-start(f32[1,4,2,128]{3,1,2,0:T(4,128)S(1)} %copy.87) | copy-start | bytes 12292
  123.3 16.0 %collective-permute-start.3 = (bf16[1408,256]{1,0:T(8,128)(2,1)}, bf16[1408,256]{1,0:T(8,128)(2,1)S(1)}, u32[]{:S(2)}, u32[]{:S(2)}) collective-permute-start(bf16[1408,256]{1,0:T(8,128)(2,1)} %collective-permute-done.1), channel_id=1, source_target_pairs={{0,28},{4,0},{8,4},{12,8},{16,12},{20,16},{24,20},{28,24},{1,29},{... | collective-permute-start | bytes 2162696 | tf_op jit(solution)/shard_map/ppermute | solution.py:20
  129.7 15.8 %collective-permute-start.4 = (bf16[1408,256]{1,0:T(8,128)(2,1)S(1)}, bf16[1408,256]{1,0:T(8,128)(2,1)S(1)}, u32[]{:S(2)}, u32[]{:S(2)}) collective-permute-start(bf16[1408,256]{1,0:T(8,128)(2,1)S(1)} %collective-permute-done.2), channel_id=1, source_target_pairs={{0,4},{4,8},{8,12},{12,16},{16,20},{20,24},{24,28},{28,0},{1,5},{5... | collective-permute-start | bytes 2162696 | tf_op jit(solution)/shard_map/ppermute | solution.py:17
  139.2 18.2 %collective-permute-start.5 = (bf16[1408,256]{1,0:T(8,128)(2,1)S(1)}, bf16[1408,256]{1,0:T(8,128)(2,1)S(1)}, u32[]{:S(2)}, u32[]{:S(2)}) collective-permute-start(bf16[1408,256]{1,0:T(8,128)(2,1)S(1)} %collective-permute-done.3), channel_id=1, source_target_pairs={{0,28},{4,0},{8,4},{12,8},{16,12},{20,16},{24,20},{28,24},{1,29},{... | collective-permute-start | bytes 2162696 | tf_op jit(solution)/shard_map/ppermute | solution.py:20
  145.5 12.9 collective-permute-start.6
  382.4 324.8 %reduce-scatter.10.cloned.1.call-start = ((), (), s32[]{:S(2)}) async-start(), calls=%async_computation.14 | async-start | bytes 294912 | tf_op jit(solution)/shard_map/reduce_scatter | solution.py:270
  633.1 75.4 %reduce-scatter.12.cloned.1.call-start = ((), (), s32[]{:S(2)}) async-start(), calls=%async_computation.15 | async-start | bytes 294912 | tf_op jit(solution)/shard_map/reduce_scatter | solution.py:273
  639.8 107.8 %reduce-scatter.8.cloned.1.call-start = ((), (), s32[]{:S(2)}) async-start(), calls=%async_computation.13 | async-start | bytes 2359296 | tf_op jit(solution)/shard_map/reduce_scatter | solution.py:267
  646.0 146.0 %reduce-scatter.14.cloned.1.call-start = ((), (), s32[]{:S(2)}) async-start(), calls=%async_computation.16 | async-start | bytes 2359296 | tf_op jit(solution)/shard_map/reduce_scatter | solution.py:276
  653.2 201.3 %reduce-scatter.18.cloned.1.call-start = ((), (), s32[]{:S(2)}) async-start(), calls=%async_computation.18 | async-start | bytes 6488064 | tf_op jit(solution)/shard_map/reduce_scatter | solution.py:282
  664.2 252.6 %reduce-scatter.16.cloned.1.call-start = ((), (), s32[]{:S(2)}) async-start(), calls=%async_computation.17 | async-start | bytes 6488064 | tf_op jit(solution)/shard_map/reduce_scatter | solution.py:279
  675.3 303.9 %reduce-scatter.20.cloned.1.call-start = ((), (), s32[]{:S(2)}) async-start(), calls=%async_computation.19 | async-start | bytes 6488064 | tf_op jit(solution)/shard_map/reduce_scatter | solution.py:285
  686.8 586.3 %all-reduce.12.cloned.1.call-start = ((), (), s32[]{:S(2)}) async-start(), calls=%async_computation.20 | async-start | bytes 16777216 | tf_op jit(solution)/shard_map/psum | solution.py:193
  705.3 567.8 %copy-start.22 = (f32[8,1,256]{2,1,0:T(1,128)S(1)}, f32[8,1,256]{2,1,0:T(1,128)}, u32[]{:S(2)}) copy-start(f32[8,1,256]{2,1,0:T(1,128)} %copy-done.21) | copy-start | bytes 24580
  705.3 567.8 %copy-start.24 = (f32[1024]{0:T(1024)S(1)}, f32[1024]{0:T(1024)}, u32[]{:S(2)}) copy-start(f32[1024]{0:T(1024)} %copy-done.23) | copy-start | bytes 12292
  (37 other events, 1054.0 us)
Sparse Core Ops, SparseCore 0:
  9.9 30.9 all-gather.6
  42.8 28.2 all-gather.8
  90.7 154.9 all-reduce.7
  247.4 42.1 all-gather.12
  291.4 43.1 all-gather.10
  382.5 154.9 all-reduce.9
  633.3 32.6 reduce-scatter.9
  669.5 33.6 reduce-scatter.11
  706.5 41.0 reduce-scatter.7
  750.8 41.1 reduce-scatter.13
  795.4 59.0 reduce-scatter.17
  857.8 59.0 reduce-scatter.15
  920.2 58.8 reduce-scatter.19
  982.2 290.8 all-reduce.11
